TPU v7x, 256 devices: a 8x8x2 block of a 8x8x16 slice. The times are simulated.
256 devices in a mesh: member: 2 (over z), lat: 128 (over x, y, core).
Axes of the slice: x: 8, y: 8, z: 2, core: 2. Of those that a mesh axis runs over, the one named last changes fastest.
The devices are a block of a 8x8x16 slice.
Arguments:
- height: float32 [1024, 32, 1440], P(('member', 'lat')), parts along dimension 0, may hold values from -6 to 6
- zonal_courant: float32 [1024, 32, 1440], P(('member', 'lat')), parts along dimension 0, may hold values from -1.5 to 1.5
- merid_courant: float32 [1024, 32, 1440], P(('member', 'lat')), parts along dimension 0, may hold values from -1.5 to 1.5
- rates: float32 [64], P('member'), parts along dimension 0, may hold values from 0.05 to 0.5
- thresholds: float32 [64], P('member'), parts along dimension 0, may hold values from -3 to 3
- flags: int32 [512], replicated, may hold values from 0 to 1, as said below
- cutoffs: int32 [512], replicated, may hold values from 45 to 360
Outputs:
- filtered_height: float32 [1024, 32, 1440], P(('member', 'lat')), parts along dimension 0
There are 2 independent parts, one for each index of `member`. A program takes and returns all parts, laid end to end along the dimension named above; an argument that names none is the same for every part. Nothing has to cross between parts.
Inputs may be any that keep to these rules, and one draw needn't show every extreme that they name: flags is 1 on a southern band of rows that starts at row 0 and on a northern band that ends at row 511, each band 512 // 8 to 128 rows long, and 0 on all other rows.
All inputs are finite; a program needn't handle non-finite values.
Results may differ from a plain program's by a relative error of at most 0.00007.
Values sent between devices are 32-bit elements; how exact they have to be, the bound alone decides.
A program may use at most 64 MiB of HBM per device.

v0:
```python
import jax
import jax.numpy as jnp
from jax import lax
from jax.sharding import Mesh
from jax.sharding import PartitionSpec as P

LAT = ("lat_0", "lat_1", "lat_2")
MEMBER_LAT = ("member", "lat_0", "lat_1", "lat_2")


def padded_2(cells, sides, width):
    for axis, dim in sides:
        count = lax.axis_size(axis)
        ends = count - 1
        head = lax.slice_in_dim(cells, 0, width, axis=dim)
        tail = lax.slice_in_dim(cells, cells.shape[dim] - width, cells.shape[dim], axis=dim)
        cells = jnp.concatenate(
            [
                lax.ppermute(tail, axis, [(i, (i + 1) % count) for i in range(ends)]),
                cells,
                lax.ppermute(head, axis, [((i + 1) % count, i) for i in range(ends)]),
            ],
            axis=dim,
        )
    return cells


def one_axis_at_a_time(array, axes):
    for axis in axes:
        array = lax.psum(array, axis)
    return array


def transform_table(nlon, nkp):
    points = jnp.arange(nlon, dtype=jnp.int32)
    waves = jnp.arange(nkp, dtype=jnp.int32)
    phase = points[:, None] * waves[None, :] % nlon
    angle = 2.0 * jnp.pi / nlon * phase.astype(jnp.float32)
    return jnp.concatenate([jnp.cos(angle), jnp.sin(angle)], axis=1)


def wave_weights(nlon, nkp):
    waves = jnp.arange(nkp, dtype=jnp.int32)
    interior = jnp.where((waves > 0) & (waves < nlon // 2), 2.0, 1.0)
    return jnp.where(waves <= nlon // 2, interior, 0.0).astype(jnp.float32) / nlon


def damping(row_flags, row_cutoffs, nkp):
    waves = jnp.maximum(jnp.arange(nkp), 1).astype(jnp.float32)
    ratio = row_cutoffs.astype(jnp.float32)[:, None] / waves[None, :]
    factor = jnp.minimum(1.0, ratio * ratio)
    return jnp.where(row_flags[:, None] > 0, factor, 1.0)


def filter_units(flat, damp, table, weights):
    highest = lax.Precision.HIGHEST
    spectrum = jnp.dot(flat, table, precision=highest, preferred_element_type=jnp.float32)
    factor = (1.0 - damp) * weights[None, :]
    scaled = spectrum * jnp.concatenate([factor, factor], axis=1)
    dims = (((1,), (1,)), ((), ()))
    removed = lax.dot_general(
        scaled, table, dims, precision=highest, preferred_element_type=jnp.float32
    )
    return flat - removed


def filtered_or_kept(block, row_flags, row_cutoffs, table, weights):
    rows, levels, nlon = block.shape
    damp = damping(row_flags, row_cutoffs, weights.shape[0])
    unit_damp = jnp.broadcast_to(damp[:, None, :], (rows, levels, damp.shape[1])).reshape(
        rows * levels, damp.shape[1]
    )

    def apply_filter(data):
        return filter_units(data.reshape(rows * levels, nlon), unit_damp, table, weights).reshape(
            rows, levels, nlon
        )

    def keep_block(data):
        return data

    return lax.cond(jnp.any(row_flags > 0), apply_filter, keep_block, block)


def face_fluxes(rows_height, rows_speed, face_cos, count):
    face_value = (
        7.0 * (rows_height[1 : count + 1] + rows_height[2 : count + 2])
        - (rows_height[0:count] + rows_height[3 : count + 3])
    ) / 12.0
    speed = 0.5 * (rows_speed[0:count] + rows_speed[1 : count + 1]) * face_cos[:, None, None]
    return speed * face_value


def face_cosines(face_ids, nlat):
    return jnp.where(
        (face_ids > 0) & (face_ids < nlat),
        jnp.sin(jnp.pi * face_ids.astype(jnp.float32) / nlat),
        jnp.float32(0.0),
    )


def local(height, zonal_courant, merid_courant, rates, thresholds, flags, cutoffs):
    lat_rows, levels, nlon = height.shape
    devices = lax.axis_size(LAT)
    position = lax.axis_index(LAT)
    first_row = position * lat_rows
    nlat = lat_rows * devices
    local_rows = first_row + jnp.arange(lat_rows, dtype=jnp.int32)
    cos_rows = jnp.sin(jnp.pi * (local_rows.astype(jnp.float32) + 0.5) / nlat)
    faces = first_row + jnp.arange(lat_rows + 1, dtype=jnp.int32)
    cos_faces = face_cosines(faces, nlat)
    padded = padded_2(jnp.stack([height, merid_courant]), ((LAT, 1),), 2)
    east = jnp.roll(height, -1, axis=2)
    west = jnp.roll(height, 1, axis=2)
    far_east = jnp.roll(height, -2, axis=2)
    face_height = (7.0 * (height + east) - (west + far_east)) / 12.0
    face_speed = 0.5 * (zonal_courant + jnp.roll(zonal_courant, -1, axis=2))
    zonal_flux = face_speed * face_height
    zonal_div = zonal_flux - jnp.roll(zonal_flux, 1, axis=2)
    source = -rates[None, :, None] * jax.nn.softplus(height - thresholds[None, :, None])
    partial_sums = jnp.sum(jnp.sum(source, axis=2) * cos_rows[:, None], axis=0)
    totals = one_axis_at_a_time(partial_sums, LAT)
    all_rows = jnp.arange(nlat, dtype=jnp.int32)
    area = nlon * jnp.sum(jnp.sin(jnp.pi * (all_rows.astype(jnp.float32) + 0.5) / nlat))
    level_mean = totals / area
    padded_height = padded[0]
    padded_speed = padded[1]
    count = lat_rows + 1
    merid_flux = face_fluxes(padded_height, padded_speed[1:], cos_faces, count)
    merid_div = (merid_flux[1:] - merid_flux[:-1]) / cos_rows[:, None, None]
    updated = height - zonal_div - merid_div + source - level_mean[None, :, None]
    nkp = (nlon // 2 + 128) // 128 * 128
    table = transform_table(nlon, nkp)
    weights = wave_weights(nlon, nkp)
    row_flags = lax.dynamic_slice_in_dim(flags, first_row, lat_rows)
    row_cutoffs = lax.dynamic_slice_in_dim(cutoffs, first_row, lat_rows)
    result = filtered_or_kept(updated, row_flags, row_cutoffs, table, weights)
    return result


def solution(mesh):
    finer = Mesh(
        mesh.devices.reshape(mesh.shape["member"], 8, 8, 2), ("member", "lat_0", "lat_1", "lat_2")
    )
    placed = (
        P(MEMBER_LAT, None, None),
        P(MEMBER_LAT, None, None),
        P(MEMBER_LAT, None, None),
        P("member"),
        P("member"),
        P(),
        P(),
    )
    return jax.shard_map(
        local, mesh=finer, in_specs=placed, out_specs=P(MEMBER_LAT, None, None), check_vma=False
    )
```

profile of v0, /device:TPU:513, one launch (start us, length us, event | category | flops | bytes accessed | tf_op | source)
XLA Modules:
  0.0 114.5 jit_solution(6825483343422072671)
XLA Ops:
  0.0 0.0 copy-start
  0.0 0.0 copy-start.2
  0.0 2.5 %fusion.17 = (f32[2,2,32,1440]{3,2,1,0:T(8,128)}, f32[2,2,32,1440]{3,2,1,0:T(8,128)S(1)}) fusion(f32[1,4,32,1440]{3,2,1,0:T(8,128)} %bitcast.21, f32[1,4,32,1440]{3,2,1,0:T(8,128)} %bitcast.27), kind=kLoop, calls=%fused_computation.33 | loop fusion | flops 368640 | bytes 2949120 | tf_op jit(solution)/shard_map/stack | solution.py:112
  2.5 5.7 %collective-permute-start = (f32[2,2,32,1440]{3,2,1,0:T(8,128)}, f32[2,2,32,1440]{3,2,1,0:T(8,128)}, u32[]{:S(2)}, u32[]{:S(2)}) collective-permute-start(f32[2,2,32,1440]{3,2,1,0:T(8,128)} %get-tuple-element.115), channel_id=1, source_target_pairs={{0,1},{1,2},{2,3},{3,4},{4,5},{5,6},{6,7},{7,8},{8,9},{9,10},{10,1... | collective-permute-start | bytes 2211848 | tf_op jit(solution)/shard_map/ppermute | solution.py:19
  8.2 18.8 %collective-permute-start.1 = (f32[2,2,32,1440]{3,2,1,0:T(8,128)S(1)}, f32[2,2,32,1440]{3,2,1,0:T(8,128)}, u32[]{:S(2)}, u32[]{:S(2)}) collective-permute-start(f32[2,2,32,1440]{3,2,1,0:T(8,128)S(1)} %get-tuple-element.116), channel_id=1, source_target_pairs={{1,0},{2,1},{3,2},{4,3},{5,4},{6,5},{7,6},{8,7},{9,8},{10,9},{11,1... | collective-permute-start | bytes 2211848 | tf_op jit(solution)/shard_map/ppermute | solution.py:21
  27.1 1.6 %fusion.33 = (f32[4,32,1439]{2,1,0:T(8,128)S(1)}, f32[4,32,1439]{2,1,0:T(8,128)S(1)}) fusion(f32[4,32,1440]{2,1,0:T(8,128)} %param.9), kind=kLoop, calls=%fused_computation.63 | loop fusion | bytes 2947072 | tf_op jit(solution)/shard_map/jit(_roll_static)/slice | solution.py:114
  28.8 0.0 copy-done
  28.8 0.1 fusion.32
  28.9 0.3 slice.95
  29.2 0.0 copy-done.2
  29.2 0.3 slice.89
  29.5 0.7 sine_reduce_fusion
  30.2 0.0 copy-start.5
  30.2 0.0 slice-start
  30.2 0.0 copy-start.4
  30.2 19.5 %fusion.7 = (f32[1440,768]{1,0:T(8,128)}, f32[1440,768]{1,0:T(8,128)}) fusion(), kind=kLoop, calls=%fused_computation.15 | loop fusion | flops 9953280 | bytes 8847360 | tf_op jit(solution)/shard_map/sin | solution.py:39
  49.7 0.0 copy-done.5
  49.7 0.0 slice-done
  49.8 0.0 copy-done.4
  49.8 0.9 fusion.29
  50.7 0.1 multiply_reduce_fusion
  50.8 10.7 %psum.21 = f32[32]{0:T(128)S(1)} all-reduce(f32[32]{0:T(128)S(1)} %multiply_reduce_fusion), channel_id=1, replica_groups=mesh['member'=2,'lat_0'=8,'lat_1'=8,'lat_2'=2] {'lat_0'}, use_global_device_ids=true, to_apply=%region_3.4 | all-reduce | flops 32 | bytes 256 | tf_op jit(solution)/shard_map/psum | solution.py:30
  61.5 10.7 %psum.22 = f32[32]{0:T(128)S(1)} all-reduce(f32[32]{0:T(128)S(1)} %psum.21), channel_id=1, replica_groups=mesh['member'=2,'lat_0'=8,'lat_1'=8,'lat_2'=2] {'lat_1'}, use_global_device_ids=true, to_apply=%region_4.5 | all-reduce | flops 32 | bytes 256 | tf_op jit(solution)/shard_map/psum | solution.py:30
  72.3 8.5 %psum.23 = f32[32]{0:T(128)S(1)} all-reduce(f32[32]{0:T(128)S(1)} %psum.22), channel_id=1, replica_groups=mesh['member'=2,'lat_0'=8,'lat_1'=8,'lat_2'=2] {'lat_2'}, use_global_device_ids=true, to_apply=%region_5.6 | all-reduce | flops 32 | bytes 256 | tf_op jit(solution)/shard_map/psum | solution.py:30
  80.7 0.1 slice.109
  80.8 1.4 %fusion.31 = (pred[]{:T(512)}, pred[4]{0:T(512)(128)(4,1)S(1)}) fusion(s32[512]{0:T(512)} %param.14, s32[]{:T(128)S(6)} %select_n.50), kind=kLoop, calls=%fused_computation.61 | loop fusion | flops 7 | bytes 25 | tf_op jit(solution)/shard_map/reduce_or | solution.py:82
  82.2 0.8 dynamic-slice_convert_fusion
  84.2 0.0 copy-start.3
  84.3 8.2 %pad_maximum_fusion = f32[1440,1536]{1,0:T(8,128)} fusion(f32[1440,768]{1,0:T(8,128)} %get-tuple-element.123, f32[1440,768]{1,0:T(8,128)} %get-tuple-element.124), kind=kLoop, calls=%fused_computation.8 | loop fusion | flops 2211840 | bytes 17694720 | tf_op jit(solution)/shard_map/concatenate | solution.py:39
  92.4 0.0 collective-permute-done
  92.4 0.0 collective-permute-done.1
  92.4 0.0 copy-done.3
  92.4 1.9 %maximum_maximum_fusion = (f32[2,6,32,1440]{3,2,1,0:T(8,128)S(1)}, f32[2,6,32,1440]{3,2,1,0:T(8,128)S(1)}) fusion(f32[1,4,32,1440]{3,2,1,0:T(8,128)S(1)} %bitcast.28, f32[1,4,32,1440]{3,2,1,0:T(8,128)S(1)} %bitcast.22, f32[2,2,32,1440]{3,2,1,0:T(8,128)} %collective-permute-done, f32[2,2,32,1440]{3,2,1,0:T(8,128)} %collective-permute-done.1), kind=kLoop, calls=%fused_computation.18 | loop fusion | flops 2211840 | bytes 7372800 | tf_op jit(solution)/shard_map/concatenate | solution.py:17
  94.4 0.5 fusion.13
  94.9 0.7 fusion.22
  95.6 18.0 %conditional.1 = (f32[4,32,1440]{2,1,0:T(8,128)S(1)}) conditional(s32[]{:T(128)} %convert_element_type.42, f32[4,32,1440]{2,1,0:T(8,128)S(1)} %fusion.22, (f32[4,32,1440]{2,1,0:T(8,128)S(1)}, f32[1440,1536]{1,0:T(8,128)}, pred[4]{0:T(512)(128)(4,1)S(1)}, f32[4]{0:T(128)S(1)}, f32[1,768]{1,0:T(1,128)S(1)}, /*index=5*/s32[768]{0:T(1024)S(1)}) %tuple.45), branch_computations={%region_7.8_spmd, %region_8.9_spmd} | conditional | flops 6795468800 | bytes 25258016 | solution.py:82
  95.9 0.1 fusion.2
  96.0 7.6 %convolution_multiply_fusion = f32[128,1536]{1,0:T(8,128)S(1)} fusion(f32[128,1440]{1,0:T(8,128)S(1)} %bitcast.24, f32[1440,1536]{1,0:T(8,128)} %get-tuple-element.105, f32[128,768]{1,0:T(8,128)S(1)} %bitcast_multiply_fusion), kind=kOutput, calls=%fused_computation.1 | convolution fusion | flops 3397779456 | bytes 10764288 | tf_op jit(solution)/shard_map/cond/branch_1_fun/dot_general | solution.py:57
  103.6 0.3 copy.27
  103.9 9.5 %convolution_subtract_fusion = f32[128,1440]{0,1:T(8,128)S(1)} fusion(f32[128,1440]{0,1:T(8,128)S(1)} %copy.27, f32[128,1536]{1,0:T(8,128)S(1)} %convolution_multiply_fusion, f32[1440,1536]{1,0:T(8,128)} %get-tuple-element.105), kind=kOutput, calls=%fused_computation | convolution fusion | flops 3397570560 | bytes 11108352 | tf_op jit(solution)/shard_map/cond/branch_1_fun/dot_general | solution.py:61
  113.4 0.3 copy.28
  113.6 0.0 copy-start.1
  113.7 0.9 copy-done.1
  (10 shorter events, 0.2 us)
Async XLA Ops:
  0.0 28.8 %copy-start = (f32[4,32,1440]{2,1,0:T(8,128)S(1)}, f32[4,32,1440]{2,1,0:T(8,128)}, u32[]{:S(2)}) copy-start(f32[4,32,1440]{2,1,0:T(8,128)} %param.9) | copy-start | bytes 2211844
  0.0 29.2 %copy-start.2 = (f32[4,32,1440]{2,1,0:T(8,128)S(1)}, f32[4,32,1440]{2,1,0:T(8,128)}, u32[]{:S(2)}) copy-start(f32[4,32,1440]{2,1,0:T(8,128)} %param.10) | copy-start | bytes 2211844
  2.5 89.9 %collective-permute-start = (f32[2,2,32,1440]{3,2,1,0:T(8,128)}, f32[2,2,32,1440]{3,2,1,0:T(8,128)}, u32[]{:S(2)}, u32[]{:S(2)}) collective-permute-start(f32[2,2,32,1440]{3,2,1,0:T(8,128)} %get-tuple-element.115), channel_id=1, source_target_pairs={{0,1},{1,2},{2,3},{3,4},{4,5},{5,6},{6,7},{7,8},{8,9},{9,10},{10,1... | collective-permute-start | bytes 2211848 | tf_op jit(solution)/shard_map/ppermute | solution.py:19
  8.2 84.2 %collective-permute-start.1 = (f32[2,2,32,1440]{3,2,1,0:T(8,128)S(1)}, f32[2,2,32,1440]{3,2,1,0:T(8,128)}, u32[]{:S(2)}, u32[]{:S(2)}) collective-permute-start(f32[2,2,32,1440]{3,2,1,0:T(8,128)S(1)} %get-tuple-element.116), channel_id=1, source_target_pairs={{1,0},{2,1},{3,2},{4,3},{5,4},{6,5},{7,6},{8,7},{9,8},{10,9},{11,1... | collective-permute-start | bytes 2211848 | tf_op jit(solution)/shard_map/ppermute | solution.py:21
  30.2 19.5 %copy-start.5 = (f32[32]{0:T(128)S(1)}, f32[32]{0:T(128)}, u32[]{:S(2)}) copy-start(f32[32]{0:T(128)} %param.12) | copy-start | bytes 388
  30.2 19.6 %slice-start = ((f32[4,32,1440]{2,1,0:T(8,128)}), f32[4,32,1]{2,1,0:T(8,128)S(1)}, s32[]{:S(2)}) async-start(f32[4,32,1440]{2,1,0:T(8,128)} %param.10), calls=%async_computation | async-start | bytes 131072 | tf_op jit(solution)/shard_map/jit(_roll_static)/slice | solution.py:117
  30.2 19.6 %copy-start.4 = (f32[32]{0:T(128)S(1)}, f32[32]{0:T(128)}, u32[]{:S(2)}) copy-start(f32[32]{0:T(128)} %param.13) | copy-start | bytes 388
  84.2 8.2 %copy-start.3 = (f32[4,32,1440]{2,1,0:T(8,128)S(1)}, f32[4,32,1440]{2,1,0:T(8,128)}, u32[]{:S(2)}) copy-start(f32[4,32,1440]{2,1,0:T(8,128)} %param.11) | copy-start | bytes 2211844
  113.6 0.9 copy-start.1
where the time goes:
time: 115 us
  other arithmetic  37.4 us (33%)
  blocking collectives  30 us (26%)
  starting transfers between devices  24.5 us (21%)
  matrix products  17.1 us (15%)
  local copies, waits for them, and re-layouts  3.78 us (3%)
  between operations  1.42 us (1%)
    psum x3, blocking collectives, one_axis_at_a_time(): array = lax.psum(array, axis)  30 us
    sin x1, other arithmetic, transform_table(): return jnp.concatenate([jnp.cos(angle), jnp.sin(angle)], axis=1)  19.5 us
    ppermute x1, starting transfers between devices, padded_2(): lax.ppermute(head, axis, [((i + 1) % count, i) for i in range(ends)])  18.8 us
    dot_general x1, matrix products, filter_units(): lax.dot_general(scaled, table, dims, precision=highest, preferred_element...  9.48 us
    concatenate x1, other arithmetic, transform_table(): return jnp.concatenate([jnp.cos(angle), jnp.sin(angle)], axis=1)  8.16 us
    dot_general x1, matrix products, filter_units(): jnp.dot(flat, table, precision=highest, preferred_element_type=jnp.float32)  7.63 us
    ppermute x1, starting transfers between devices, padded_2(): lax.ppermute(tail, axis, [(i, (i + 1) % count) for i in range(ends)])  5.73 us
    another operation x1, other arithmetic, local(): padded = padded_2(jnp.stack([height, merid_courant]), ((LAT, 1),), 2)  2.49 us
  transfers between devices with their start and end apart: 2, of which 0 were waited for; matrix products, arithmetic and copies ran while one was open for 30% of the time, Pallas kernels for 0%

commit v1 on v0

--- a/solution.py
+++ b/solution.py
@@ -27,7 +27,7 @@
 
 def one_axis_at_a_time(array, axes):
     for axis in axes:
-        array = lax.psum(array, axis)
+        array = jnp.sum(lax.all_gather(array, axis), axis=0)
     return array
 
 

time: 115 us -> 124 us (1.078)
  local copies, waits for them, and re-layouts: 3.78 us -> 8.89 us
  between operations: 1.42 us -> 3.59 us
  other arithmetic: 37.4 us -> 39.4 us
    psum x3 -> x0, blocking collectives: 30 us -> none  [one_axis_at_a_time(): array = lax.psum(array, axis)]
    unnamed x0 -> x3, blocking collectives: none -> 29.9 us
    unnamed x12 -> x29, local copies, waits for them, and re-layouts: 0.9 us -> 3.65 us
    reduce_sum x2, other arithmetic: 1 us -> 2.59 us  [local(): partial_sums = jnp.sum(jnp.sum(source, axis=2) * cos_rows[:, None], axis=0)]
  transfers between devices with their start and end apart: 2 -> 2, of which waited for: 0 -> 0; matrix products, arithmetic and copies ran while one was open for 30% -> 33% of each run, Pallas kernels for 0% -> 0%
where the time goes in v1:
time: 124 us
  other arithmetic  39.4 us (32%)
  blocking collectives  29.9 us (24%)
  starting transfers between devices  24.5 us (20%)
  matrix products  17.1 us (14%)
  local copies, waits for them, and re-layouts  8.89 us (7%)
  between operations  3.59 us (3%)
    unnamed x3, blocking collectives  29.9 us
    sin x1, other arithmetic, transform_table(): return jnp.concatenate([jnp.cos(angle), jnp.sin(angle)], axis=1)  19.5 us
    ppermute x1, starting transfers between devices, padded_2(): lax.ppermute(head, axis, [((i + 1) % count, i) for i in range(ends)])  18.8 us
    dot_general x1, matrix products, filter_units(): lax.dot_general(scaled, table, dims, precision=highest, preferred_element...  9.48 us
    concatenate x1, other arithmetic, transform_table(): return jnp.concatenate([jnp.cos(angle), jnp.sin(angle)], axis=1)  8.16 us
    dot_general x1, matrix products, filter_units(): jnp.dot(flat, table, precision=highest, preferred_element_type=jnp.float32)  7.63 us
    ppermute x1, starting transfers between devices, padded_2(): lax.ppermute(tail, axis, [(i, (i + 1) % count) for i in range(ends)])  5.73 us
    unnamed x29, local copies, waits for them, and re-layouts  3.65 us
  transfers between devices with their start and end apart: 2, of which 0 were waited for; matrix products, arithmetic and copies ran while one was open for 33% of the time, Pallas kernels for 0%

profile of v1, /device:TPU:513, one launch (start us, length us, event | category | flops | bytes accessed | tf_op | source)
XLA Modules:
  0.0 123.6 jit_solution(6235333459923784840)
XLA Ops:
  0.0 0.0 copy-start
  0.0 0.0 copy-start.2
  0.0 2.7 %fusion.17 = (f32[2,2,32,1440]{3,2,1,0:T(8,128)}, f32[2,2,32,1440]{3,2,1,0:T(8,128)}) fusion(f32[1,4,32,1440]{3,2,1,0:T(8,128)} %bitcast.24, f32[1,4,32,1440]{3,2,1,0:T(8,128)} %bitcast.30), kind=kLoop, calls=%fused_computation.33 | loop fusion | flops 368640 | bytes 2949120 | tf_op jit(solution)/shard_map/stack | solution.py:112
  2.8 5.7 %collective-permute-start = (f32[2,2,32,1440]{3,2,1,0:T(8,128)}, f32[2,2,32,1440]{3,2,1,0:T(8,128)}, u32[]{:S(2)}, u32[]{:S(2)}) collective-permute-start(f32[2,2,32,1440]{3,2,1,0:T(8,128)} %get-tuple-element.115), channel_id=1, source_target_pairs={{0,1},{1,2},{2,3},{3,4},{4,5},{5,6},{6,7},{7,8},{8,9},{9,10},{10,1... | collective-permute-start | bytes 2211848 | tf_op jit(solution)/shard_map/ppermute | solution.py:19
  8.5 18.8 %collective-permute-start.1 = (f32[2,2,32,1440]{3,2,1,0:T(8,128)}, f32[2,2,32,1440]{3,2,1,0:T(8,128)}, u32[]{:S(2)}, u32[]{:S(2)}) collective-permute-start(f32[2,2,32,1440]{3,2,1,0:T(8,128)} %get-tuple-element.116), channel_id=1, source_target_pairs={{1,0},{2,1},{3,2},{4,3},{5,4},{6,5},{7,6},{8,7},{9,8},{10,9},{11,1... | collective-permute-start | bytes 2211848 | tf_op jit(solution)/shard_map/ppermute | solution.py:21
  27.3 2.9 %fusion.33 = (f32[4,32,1439]{2,1,0:T(8,128)}, f32[4,32,1439]{2,1,0:T(8,128)}) fusion(f32[4,32,1440]{2,1,0:T(8,128)} %param.9), kind=kLoop, calls=%fused_computation.63 | loop fusion | bytes 2947072 | tf_op jit(solution)/shard_map/jit(_roll_static)/slice | solution.py:114
  30.1 0.0 copy-done
  30.2 0.1 fusion.32
  30.2 0.3 slice.95
  30.5 0.0 copy-done.2
  30.5 1.2 slice.89
  31.7 0.6 sine_reduce_fusion
  32.4 0.0 copy-start.6
  32.4 0.0 copy-start.3
  32.5 0.0 slice-start
  32.5 0.0 copy-start.5
  32.5 19.5 %fusion.7 = (f32[1440,768]{1,0:T(8,128)}, f32[1440,768]{1,0:T(8,128)}) fusion(), kind=kLoop, calls=%fused_computation.15 | loop fusion | flops 9953280 | bytes 8847360 | tf_op jit(solution)/shard_map/sin | solution.py:39
  52.0 0.0 copy-start.9
  52.0 0.0 copy-start.8
  52.0 0.0 copy-start.7
  52.0 0.0 copy-done.6
  52.1 0.0 copy-done.3
  52.1 0.0 slice-done
  52.1 0.0 copy-done.5
  52.1 2.5 %fusion.29 = (f32[4,32]{1,0:T(4,128)S(1)}, f32[4,32,1440]{2,1,0:T(8,128)S(1)}) fusion(f32[4,32,1440]{2,1,0:T(8,128)S(1)} %copy-done, f32[32]{0:T(128)S(1)} %copy-done.5, f32[32]{0:T(128)S(1)} %neg.8, f32[4,32,2]{2,1,0:T(8,128)S(1)} %slice.96, f32[4,32,1438]{2,1,0:T(8,128)S(1)} %slice.95, f32[4,32,1439]{2,1,0:T(8,128)} %get-tuple-element.121, ...), kind=kLoop, calls=%fused_computation.51 | loop fusion | flops 3870592 | bytes 5161728 | tf_op jit(solution)/shard_map/reduce_sum | solution.py:121
  54.6 0.1 multiply_reduce_fusion
  54.7 0.0 copy-done.9
  54.7 0.7 dynamic-slice
  56.1 0.2 dynamic-update-slice
  56.3 10.7 %all-reduce = f32[256]{0:T(256)S(1)} all-reduce(f32[256]{0:T(256)S(1)} %dynamic-update-slice), channel_id=2, replica_groups=mesh['member'=2,'lat_0'=8,'lat_1'=8,'lat_2'=2] {'lat_0'}, use_global_device_ids=true, to_apply=%add | all-reduce | flops 256 | bytes 2048
  67.0 0.1 reshape.117
  67.1 0.0 copy-done.8
  67.1 0.7 dynamic-slice.1
  68.5 0.2 dynamic-update-slice.1
  68.7 10.7 %all-reduce.1 = f32[256]{0:T(256)S(1)} all-reduce(f32[256]{0:T(256)S(1)} %dynamic-update-slice.1), channel_id=3, replica_groups=mesh['member'=2,'lat_0'=8,'lat_1'=8,'lat_2'=2] {'lat_1'}, use_global_device_ids=true, to_apply=%add.1 | all-reduce | flops 256 | bytes 2048
  79.5 0.1 reshape.118
  79.5 0.0 copy-done.7
  79.5 0.7 dynamic-slice.2
  80.9 0.2 dynamic-update-slice.2
  81.2 8.5 %all-reduce.2 = f32[64]{0:T(128)S(1)} all-reduce(f32[64]{0:T(128)S(1)} %dynamic-update-slice.2), channel_id=4, replica_groups=mesh['member'=2,'lat_0'=8,'lat_1'=8,'lat_2'=2] {'lat_2'}, use_global_device_ids=true, to_apply=%add.2 | all-reduce | flops 64 | bytes 512
  89.6 0.1 reshape.119
  89.7 0.1 slice.109
  89.8 1.5 %fusion.31 = (pred[]{:T(512)}, pred[4]{0:T(512)(128)(4,1)S(1)}) fusion(s32[512]{0:T(512)} %param.14, s32[]{:T(128)S(6)} %select_n.50), kind=kLoop, calls=%fused_computation.61 | loop fusion | flops 7 | bytes 25 | tf_op jit(solution)/shard_map/reduce_or | solution.py:82
  91.3 0.8 dynamic-slice_convert_fusion
  93.3 0.0 copy-start.4
  93.3 8.2 %pad_maximum_fusion = f32[1440,1536]{1,0:T(8,128)} fusion(f32[1440,768]{1,0:T(8,128)} %get-tuple-element.123, f32[1440,768]{1,0:T(8,128)} %get-tuple-element.124), kind=kLoop, calls=%fused_computation.8 | loop fusion | flops 2211840 | bytes 17694720 | tf_op jit(solution)/shard_map/concatenate | solution.py:39
  101.5 0.0 collective-permute-done
  101.5 0.0 collective-permute-done.1
  101.5 0.0 copy-done.4
  101.5 1.9 %maximum_maximum_fusion = (f32[2,6,32,1440]{3,2,1,0:T(8,128)S(1)}, f32[2,6,32,1440]{3,2,1,0:T(8,128)S(1)}) fusion(f32[1,4,32,1440]{3,2,1,0:T(8,128)S(1)} %bitcast.31, f32[1,4,32,1440]{3,2,1,0:T(8,128)S(1)} %bitcast.25, f32[2,2,32,1440]{3,2,1,0:T(8,128)} %collective-permute-done, f32[2,2,32,1440]{3,2,1,0:T(8,128)} %collective-permute-done.1), kind=kLoop, calls=%fused_computation.18 | loop fusion | flops 2211840 | bytes 7372800 | tf_op jit(solution)/shard_map/concatenate | solution.py:17
  103.5 0.5 fusion.13
  104.0 0.7 fusion.22
  104.7 18.0 %conditional.1 = (f32[4,32,1440]{2,1,0:T(8,128)S(1)}) conditional(s32[]{:T(128)} %convert_element_type.42, f32[4,32,1440]{2,1,0:T(8,128)S(1)} %fusion.22, (f32[4,32,1440]{2,1,0:T(8,128)S(1)}, f32[1440,1536]{1,0:T(8,128)}, pred[4]{0:T(512)(128)(4,1)S(1)}, f32[4]{0:T(128)S(1)}, f32[1,768]{1,0:T(1,128)S(1)}, /*index=5*/s32[768]{0:T(1024)S(1)}) %tuple.45), branch_computations={%region_7.8_spmd, %region_8.9_spmd} | conditional | flops 6795468800 | bytes 25258016 | solution.py:82
  104.9 0.1 fusion.2
  105.1 7.6 %convolution_multiply_fusion = f32[128,1536]{1,0:T(8,128)S(1)} fusion(f32[128,1440]{1,0:T(8,128)S(1)} %bitcast.27, f32[1440,1536]{1,0:T(8,128)} %get-tuple-element.105, f32[128,768]{1,0:T(8,128)S(1)} %bitcast_multiply_fusion), kind=kOutput, calls=%fused_computation.1 | convolution fusion | flops 3397779456 | bytes 10764288 | tf_op jit(solution)/shard_map/cond/branch_1_fun/dot_general | solution.py:57
  112.7 0.3 copy.27
  113.0 9.5 %convolution_subtract_fusion = f32[128,1440]{0,1:T(8,128)S(1)} fusion(f32[128,1440]{0,1:T(8,128)S(1)} %copy.27, f32[128,1536]{1,0:T(8,128)S(1)} %convolution_multiply_fusion, f32[1440,1536]{1,0:T(8,128)} %get-tuple-element.105), kind=kOutput, calls=%fused_computation | convolution fusion | flops 3397570560 | bytes 11108352 | tf_op jit(solution)/shard_map/cond/branch_1_fun/dot_general | solution.py:61
  122.5 0.3 copy.28
  122.7 0.0 copy-start.1
  122.7 0.9 copy-done.1
  (16 shorter events, 0.2 us)
Async XLA Ops:
  0.0 30.2 %copy-start = (f32[4,32,1440]{2,1,0:T(8,128)S(1)}, f32[4,32,1440]{2,1,0:T(8,128)}, u32[]{:S(2)}) copy-start(f32[4,32,1440]{2,1,0:T(8,128)} %param.9) | copy-start | bytes 2211844
  0.0 30.5 %copy-start.2 = (f32[4,32,1440]{2,1,0:T(8,128)S(1)}, f32[4,32,1440]{2,1,0:T(8,128)}, u32[]{:S(2)}) copy-start(f32[4,32,1440]{2,1,0:T(8,128)} %param.10) | copy-start | bytes 2211844
  2.8 98.7 %collective-permute-start = (f32[2,2,32,1440]{3,2,1,0:T(8,128)}, f32[2,2,32,1440]{3,2,1,0:T(8,128)}, u32[]{:S(2)}, u32[]{:S(2)}) collective-permute-start(f32[2,2,32,1440]{3,2,1,0:T(8,128)} %get-tuple-element.115), channel_id=1, source_target_pairs={{0,1},{1,2},{2,3},{3,4},{4,5},{5,6},{6,7},{7,8},{8,9},{9,10},{10,1... | collective-permute-start | bytes 2211848 | tf_op jit(solution)/shard_map/ppermute | solution.py:19
  8.5 93.0 %collective-permute-start.1 = (f32[2,2,32,1440]{3,2,1,0:T(8,128)}, f32[2,2,32,1440]{3,2,1,0:T(8,128)}, u32[]{:S(2)}, u32[]{:S(2)}) collective-permute-start(f32[2,2,32,1440]{3,2,1,0:T(8,128)} %get-tuple-element.116), channel_id=1, source_target_pairs={{1,0},{2,1},{3,2},{4,3},{5,4},{6,5},{7,6},{8,7},{9,8},{10,9},{11,1... | collective-permute-start | bytes 2211848 | tf_op jit(solution)/shard_map/ppermute | solution.py:21
  32.4 19.6 %copy-start.6 = (f32[32]{0:T(128)S(1)}, f32[32]{0:T(128)}, u32[]{:S(2)}) copy-start(f32[32]{0:T(128)} %param.12) | copy-start | bytes 388
  32.4 19.6 %copy-start.3 = (f32[4,32,1440]{2,1,0:T(8,128)S(1)}, f32[4,32,1440]{2,1,0:T(8,128)}, u32[]{:S(2)}) copy-start(f32[4,32,1440]{2,1,0:T(8,128)} %param.10) | copy-start | bytes 2211844
  32.5 19.6 %slice-start = ((f32[4,32,1440]{2,1,0:T(8,128)}), f32[4,32,1]{2,1,0:T(8,128)S(1)}, s32[]{:S(2)}) async-start(f32[4,32,1440]{2,1,0:T(8,128)} %param.10), calls=%async_computation | async-start | bytes 131072 | tf_op jit(solution)/shard_map/jit(_roll_static)/slice | solution.py:117
  32.5 19.6 %copy-start.5 = (f32[32]{0:T(128)S(1)}, f32[32]{0:T(128)}, u32[]{:S(2)}) copy-start(f32[32]{0:T(128)} %param.13) | copy-start | bytes 388
  52.0 2.7 %copy-start.9 = (u32[256]{0:T(256)S(1)}, u32[256]{0:T(256)}, u32[]{:S(2)}) copy-start(u32[256]{0:T(256)} %constant.107) | copy-start | bytes 3076
  52.0 15.1 %copy-start.8 = (u32[256]{0:T(256)S(1)}, u32[256]{0:T(256)}, u32[]{:S(2)}) copy-start(u32[256]{0:T(256)} %constant.112) | copy-start | bytes 3076
  52.0 27.5 %copy-start.7 = (u32[256]{0:T(256)S(1)}, u32[256]{0:T(256)}, u32[]{:S(2)}) copy-start(u32[256]{0:T(256)} %constant.117) | copy-start | bytes 3076
  93.3 8.2 %copy-start.4 = (f32[4,32,1440]{2,1,0:T(8,128)S(1)}, f32[4,32,1440]{2,1,0:T(8,128)}, u32[]{:S(2)}) copy-start(f32[4,32,1440]{2,1,0:T(8,128)} %param.11) | copy-start | bytes 2211844
  122.7 0.9 copy-start.1
